TPU v7x, 32 devices: a whole 2x2x4 slice. The times are simulated.
32 devices in a mesh: seq: 8 (over z, x), head: 4 (over y, core).
Axes of the slice: x: 2, y: 2, z: 4, core: 2. Of those that a mesh axis runs over, the one named last changes fastest.
Arguments:
- query_rows: bfloat16 [16384, 1024], P('seq', 'head'), may hold values from -8 to 8
- key_rows: bfloat16 [16384, 1024], P('seq', 'head'), may hold values from -6 to 6
- value_rows: bfloat16 [16384, 1024], P('seq', 'head'), may hold values from -12 to 12
- out_grad: bfloat16 [16384, 1024], P('seq', 'head'), may hold values from -12 to 12
- block_perm: int32 [8, 64], P('head'), may hold values from 0 to 63, as said below
- cut_count: int32 [8], P('head'), may hold values from 1 to 4, as said below
- norm_gain: float32 [1024], P('head'), may hold values from 0.1 to 1.9
Outputs:
- normed_out: bfloat16 [16384, 1024], P('seq', 'head')
- query_grad: bfloat16 [16384, 1024], P('seq', 'head')
- key_grad: bfloat16 [16384, 1024], P('seq', 'head')
- value_grad: bfloat16 [16384, 1024], P('seq', 'head')
- gain_grad: float32 [1024], P('head')
Inputs may be any that keep to these rules, and one draw needn't show every extreme that they name: `block_perm`: each row is a permutation of 0 to 63. For every head, of the 8 blocks d * 8 to (d + 1) * 8 - 1, at most 1 are paired with blocks of one range s * 8 to (s + 1) * 8 - 1, and some pair (d, s) reaches 1. `cut_count`: some head has exactly 4.
All inputs are finite; a program needn't handle non-finite values.
Results may differ from a plain program's by a relative error of at most 0.0071.
Values may be sent and summed in bfloat16 or wider, within the bound.
A program may use at most 128 MiB of HBM per device.

v0:
```python
import math

import jax
import jax.numpy as jnp
from jax import lax
from jax.experimental import pallas as pl
from jax.experimental.pallas import tpu as pltpu
from jax.sharding import PartitionSpec as P

BLOCK = 256
KCUT = 4
F32 = jnp.float32
BF16 = jnp.bfloat16
NT = (((1,), (1,)), ((), ()))
TN = (((0,), (0,)), ((), ()))
NN = (((1,), (0,)), ((), ()))
VMEM_LIMIT = 60 * 1024 * 1024
MESH = pl.DeviceIdType.MESH


def dot(a, b, dims):
    return lax.dot_general(a, b, dims, preferred_element_type=F32)


class Dims:
    def __init__(self, heads, width, blocks, slots, head_devs):
        self.heads = heads
        self.width = width
        self.blocks = blocks
        self.slots = slots
        self.head_devs = head_devs
        self.inner = 2
        self.outer = slots // 2
        self.stat_rows = 8 * (-(-2 * heads // 8))


def scratch_of(d):
    H, W, NB, S, L = d.heads, d.width, d.blocks, d.slots, d.outer
    dma = pltpu.SemaphoreType.DMA
    return dict(
        q=pltpu.VMEM((NB, BLOCK, H * W), BF16),
        k=pltpu.VMEM((NB, BLOCK, H * W), BF16),
        v=pltpu.VMEM((NB, BLOCK, H * W), BF16),
        g=pltpu.VMEM((NB, BLOCK, H * W), BF16),
        kv_send=pltpu.VMEM((S, H, BLOCK, 2 * W), BF16),
        kv_recv=pltpu.VMEM((S, H, BLOCK, 2 * W), BF16),
        cut=pltpu.VMEM((S, H, BLOCK, 2 * W), BF16),
        q_send=pltpu.VMEM((S, H, BLOCK, W), BF16),
        q_recv=pltpu.VMEM((S, H, BLOCK, W), BF16),
        cot_send=pltpu.VMEM((S, H, BLOCK, W), BF16),
        cot_recv=pltpu.VMEM((S, H, BLOCK, W), BF16),
        cst_send=pltpu.VMEM((S, d.stat_rows, BLOCK), F32),
        cst_recv=pltpu.VMEM((S, d.stat_rows, BLOCK), F32),
        ck=pltpu.VMEM((H, KCUT * BLOCK, W), BF16),
        cv=pltpu.VMEM((H, KCUT * BLOCK, W), BF16),
        s_buf=pltpu.VMEM((H, 1 + KCUT, BLOCK, BLOCK), F32),
        acc=pltpu.VMEM((H, NB, W, BLOCK), F32),
        soft=pltpu.VMEM((H, NB, 8, BLOCK), F32),
        attn_t=pltpu.VMEM((H, NB, W, BLOCK), BF16),
        g_t=pltpu.VMEM((H, NB, W, BLOCK), BF16),
        gain_t=pltpu.VMEM((H, W, BLOCK), F32),
        gain_acc=pltpu.VMEM((H, W, BLOCK), F32),
        sum_mine=pltpu.VMEM((2 * NB, BLOCK), F32),
        sum_recv=pltpu.VMEM((d.head_devs, 2 * NB, BLOCK), F32),
        row=pltpu.VMEM((2 * NB, BLOCK), F32),
        stat=pltpu.VMEM((NB, d.stat_rows, BLOCK), F32),
        cot=pltpu.VMEM((H, NB, BLOCK, W), BF16),
        cut_sum=pltpu.VMEM((H, KCUT, BLOCK, 2 * W), F32),
        x_send=pltpu.VMEM((H, L, BLOCK, 2 * W), BF16),
        x_recv=pltpu.VMEM((H, L, BLOCK, 2 * W), BF16),
        z_send=pltpu.VMEM((H, L, BLOCK, 2 * W), BF16),
        z_recv=pltpu.VMEM((H, L, BLOCK, 2 * W), BF16),
        dkv=pltpu.VMEM((NB, H, BLOCK, 2 * W), F32),
        gain_mine=pltpu.VMEM((8, H * W), F32),
        gain_recv=pltpu.VMEM((S, 8, H * W), F32),
        norm_buf=pltpu.VMEM((NB, BLOCK, H * W), BF16),
        dq_buf=pltpu.VMEM((NB, BLOCK, H * W), BF16),
        dk_buf=pltpu.VMEM((NB, BLOCK, H * W), BF16),
        dv_buf=pltpu.VMEM((NB, BLOCK, H * W), BF16),
        in_sem=dma((4,)),
        out_sem=dma((4,)),
        own_sem=dma((4,)),
        kv_ss=dma((S,)),
        kv_rs=dma((S,)),
        q_ss=dma((S,)),
        q_rs=dma((S,)),
        cot_ss=dma((S,)),
        cot_rs=dma((S,)),
        cst_ss=dma((S,)),
        cst_rs=dma((S,)),
        up_ss=dma((L,)),
        down_ss=dma((L,)),
        across_ss=dma((L,)),
        cut_rs=dma((S,)),
        sum_ss=dma((d.head_devs,)),
        sum_rs=dma((d.head_devs,)),
        x_ss=dma((H,)),
        x_rs=dma((H,)),
        z_ss=dma((H, L)),
        z_rs=dma((H, L)),
        gain_ss=dma((S,)),
        gain_rs=dma((S,)),
    )


def make_kernel(d, names):
    H, W, NB, S, L, HD = d.heads, d.width, d.blocks, d.slots, d.outer, d.head_devs
    features = HD * H * W
    scale = W ** (-0.5)
    factor = scale * math.log2(math.e)

    def cols(h):
        return slice(h * W, (h + 1) * W)

    def kernel(perm, count, q_hbm, k_hbm, v_hbm, g_hbm, gain, norm_hbm, dq_hbm, dk_hbm, dv_hbm, gain_out, *scratch):
        m = dict(zip(names, scratch))
        pos = lax.axis_index("seq")
        hpos = lax.axis_index("head")
        o = lax.div(pos, 2)
        i = lax.rem(pos, 2)

        def local(src, dst, sem):
            return pltpu.make_async_copy(src, dst, sem)

        def remote(src, dst, ss, rs, seq=None, head=None):
            target = {"seq": seq} if seq is not None else {"head": head}
            return pltpu.make_async_remote_copy(
                src_ref=src, dst_ref=dst, send_sem=ss, recv_sem=rs, device_id=target, device_id_type=MESH
            )

        loads = [
            local(src, m[name], m["in_sem"].at[n])
            for n, (src, name) in enumerate([(k_hbm, "k"), (v_hbm, "v"), (q_hbm, "q"), (g_hbm, "g")])
        ]
        for copy in loads:
            copy.start()

        barrier = pltpu.get_barrier_semaphore()
        for n in range(1, S):
            pl.semaphore_signal(barrier, inc=1, device_id={"seq": lax.rem(pos + n, S)}, device_id_type=MESH)
        for n in range(1, HD):
            pl.semaphore_signal(barrier, inc=1, device_id={"head": lax.rem(hpos + n, HD)}, device_id_type=MESH)

        kv_idx = []
        q_idx = []
        slot_of = []
        for h in range(H):
            kv_row = []
            q_row = []
            slot_row = []
            for s in range(S):
                idx = jnp.int32(0)
                qi = jnp.int32(0)
                valid = jnp.int32(-1)
                for b in range(NB):
                    p = perm[h, s * NB + b]
                    mine = lax.div(p, NB) == pos
                    idx = jnp.where(mine, lax.rem(p, NB), idx)
                    valid = jnp.where(mine, lax.rem(p, NB), valid)
                    there = lax.div(perm[h, pos * NB + b], NB) == s
                    qi = jnp.where(there, b, qi)
                slot_row.append(valid)
                kv_row.append(idx)
                q_row.append(qi)
            kv_idx.append(kv_row)
            q_idx.append(q_row)
            slot_of.append(slot_row)
        cut_dev = [[lax.div(perm[h, c], NB) for c in range(KCUT)] for h in range(H)]
        cut_local = []
        cut_has = []
        closed = []
        for h in range(H):
            where = jnp.int32(0)
            has = jnp.int32(0)
            for c in range(KCUT):
                mine = cut_dev[h][c] == pos
                where = jnp.where(mine, lax.rem(perm[h, c], NB), where)
                has = jnp.where(mine, 1, has)
            cut_local.append(where)
            cut_has.append(has)
            closed.append([jnp.where(count[h] > c, jnp.float32(0), jnp.float32(1e30)) for c in range(KCUT)])

        loads[0].wait()
        loads[1].wait()
        k, v, q, g = m["k"], m["v"], m["q"], m["g"]
        for h in range(H):
            r = cut_local[h]
            m["cut"][pos, h, :, :W] = k[r, :, cols(h)]
            m["cut"][pos, h, :, W:] = v[r, :, cols(h)]
        for h in range(H):
            for s in range(S):
                r = kv_idx[h][s]
                m["kv_send"][s, h, :, :W] = k[r, :, cols(h)]
                m["kv_send"][s, h, :, W:] = v[r, :, cols(h)]
        pl.semaphore_wait(barrier, S - 1 + HD - 1)

        def cut_copy(outer, sem, target):
            slot = outer * 2 + i
            return remote(m["cut"].at[slot], m["cut"].at[slot], sem, m["cut_rs"].at[slot], seq=target)

        def cut_arrive(slot):
            remote(m["cut"].at[slot], m["cut"].at[slot], m["across_ss"].at[0], m["cut_rs"].at[slot], seq=pos).wait_recv()

        def kv_copy(n):
            peer = lax.rem(pos + n, S)
            return remote(m["kv_send"].at[peer], m["kv_recv"].at[pos], m["kv_ss"].at[n], m["kv_rs"].at[n], seq=peer)

        def q_copy(n):
            peer = lax.rem(pos + n, S)
            return remote(m["q_send"].at[peer], m["q_recv"].at[pos], m["q_ss"].at[n], m["q_rs"].at[n], seq=peer)

        def arrive(buf, rs, n):
            src = lax.rem(pos + S - n, S)
            remote(m[buf].at[src], m[buf].at[src], m[rs].at[n], m[rs].at[n], seq=src).wait_recv()

        has_up = o + 1 < L
        has_down = o > 0

        def up(t):
            return cut_copy(o - t, m["up_ss"].at[t], pos + 2)

        def down(t):
            return cut_copy(o + t, m["down_ss"].at[t], pos - 2)

        def across(outer):
            return cut_copy(outer, m["across_ss"].at[outer], o * 2 + 1 - i)

        per = -(-(S - 1) // L)
        groups = [list(range(1, S))[n * per : (n + 1) * per] for n in range(L)]

        pl.when(has_up)(lambda: up(0).start())
        pl.when(has_down)(lambda: down(0).start())
        across(o).start()
        for n in groups[0]:
            kv_copy(n).start()
        own_kv = local(m["kv_send"].at[pos], m["kv_recv"].at[pos], m["own_sem"].at[0])
        own_kv.start()

        loads[2].wait()
        for h in range(H):
            for s in range(S):
                m["q_send"][s, h] = q[q_idx[h][s], :, cols(h)]
        own_q = local(m["q_send"].at[pos], m["q_recv"].at[pos], m["own_sem"].at[1])
        own_q.start()
        loads[3].wait()
        for h in range(H):
            m["gain_t"][h] = jnp.broadcast_to(gain[:, cols(h)], (BLOCK, W)).T
            m["gain_acc"][h] = jnp.zeros((W, BLOCK), F32)

        def turn(b, carry):
            for h in range(H):
                m["g_t"][h, b] = g[b, :, cols(h)].astype(F32).T.astype(BF16)
            return carry

        lax.fori_loop(0, NB, turn, 0)

        for t in range(L - 1):
            below = o - 1 - t
            above = o + 1 + t

            @pl.when(below >= 0)
            def _(below=below, t=t):
                cut_arrive(below * 2 + i)
                pl.when(has_up)(lambda: up(t + 1).start())
                across(below).start()

            @pl.when(above < L)
            def _(above=above, t=t):
                cut_arrive(above * 2 + i)
                pl.when(has_down)(lambda: down(t + 1).start())
                across(above).start()

            for n in groups[t + 1]:
                kv_copy(n).start()
        for n in range(1, S):
            q_copy(n).start()
        for outer in range(L):
            cut_arrive(outer * 2 + 1 - i)
        for h in range(H):
            for c in range(KCUT):
                m["ck"][h, c * BLOCK : (c + 1) * BLOCK] = m["cut"][cut_dev[h][c], h, :, :W]
                m["cv"][h, c * BLOCK : (c + 1) * BLOCK] = m["cut"][cut_dev[h][c], h, :, W:]

        def part_a(b, carry):
            for h in range(H):
                query = q[b, :, cols(h)]
                s = dot(k[b, :, cols(h)], query, NT)
                m["s_buf"][h, 0] = s
                top = jnp.max(s, axis=0, keepdims=True) * factor
                for c in range(KCUT):
                    s = dot(m["ck"][h, c * BLOCK : (c + 1) * BLOCK], query, NT)
                    m["s_buf"][h, 1 + c] = s
                    top = jnp.maximum(top, jnp.max(s, axis=0, keepdims=True) * factor - closed[h][c])
                e = jnp.exp2(m["s_buf"][h, 0] * factor - top)
                total = jnp.sum(e, axis=0, keepdims=True)
                acc = dot(v[b, :, cols(h)], e.astype(BF16), TN)
                for c in range(KCUT):
                    e = jnp.exp2(m["s_buf"][h, 1 + c] * factor - (top + closed[h][c]))
                    total = total + jnp.sum(e, axis=0, keepdims=True)
                    acc = acc + dot(m["cv"][h, c * BLOCK : (c + 1) * BLOCK], e.astype(BF16), TN)
                m["acc"][h, b] = acc
                m["soft"][h, b] = jnp.concatenate([top, total, jnp.zeros((6, BLOCK), F32)], axis=0)
            return carry

        lax.fori_loop(0, NB, part_a, 0)

        own_kv.wait()
        for n in range(1, S):
            arrive("kv_recv", "kv_rs", n)

        def part_b(b, carry):
            square = jnp.zeros((1, BLOCK), F32)
            mix = jnp.zeros((1, BLOCK), F32)
            for h in range(H):
                slot = lax.div(perm[h, pos * NB + b], NB)
                query = q[b, :, cols(h)]
                s = dot(m["kv_recv"][slot, h, :, :W], query, NT)
                soft = m["soft"][h, b]
                old = soft[0:1]
                top = jnp.maximum(old, jnp.max(s, axis=0, keepdims=True) * factor)
                alpha = jnp.exp2(old - top)
                e = jnp.exp2(s * factor - top)
                total = soft[1:2] * alpha + jnp.sum(e, axis=0, keepdims=True)
                acc = m["acc"][h, b] * alpha + dot(m["kv_recv"][slot, h, :, W:], e.astype(BF16), TN)
                attn = (acc / total).astype(BF16)
                m["attn_t"][h, b] = attn
                attn = attn.astype(F32)
                lse = top + jnp.log2(total)
                m["soft"][h, b] = jnp.concatenate([lse, jnp.zeros((7, BLOCK), F32)], axis=0)
                square = square + jnp.sum(attn * attn, axis=0, keepdims=True)
                mix = mix + jnp.sum(
                    m["gain_t"][h] * m["g_t"][h, b].astype(F32) * attn, axis=0, keepdims=True
                )
            m["sum_mine"][pl.ds(b, 1), :] = square
            m["sum_mine"][pl.ds(NB + b, 1), :] = mix
            return carry

        lax.fori_loop(0, NB, part_b, 0)

        def sum_copy(n):
            return remote(
                m["sum_mine"], m["sum_recv"].at[n], m["sum_ss"].at[n], m["sum_rs"].at[n], head=lax.rem(hpos + n, HD)
            )

        for n in range(1, HD):
            sum_copy(n).start()
        sums = m["sum_mine"][...]
        for n in range(1, HD):
            sum_copy(n).wait_recv()
        for n in range(1, HD):
            sums = sums + m["sum_recv"][n]
        scale_rows = lax.rsqrt(sums[:NB] / features + 1e-06)
        m["row"][:NB] = scale_rows
        m["row"][NB:] = scale_rows * scale_rows * scale_rows * sums[NB:] / features

        def part_c(b, carry):
            scale_row = m["row"][pl.ds(b, 1), :]
            coef = m["row"][pl.ds(NB + b, 1), :]
            pieces = []
            for h in range(H):
                attn = m["attn_t"][h, b].astype(F32)
                grad = m["g_t"][h, b].astype(F32)
                gain_t = m["gain_t"][h]
                scaled = attn * scale_row
                m["norm_buf"][b, :, cols(h)] = (scaled * gain_t).T.astype(BF16)
                cot = (scale_row * gain_t * grad - attn * coef).astype(BF16).astype(F32)
                m["cot"][h, b] = cot.T.astype(BF16)
                delta = jnp.sum(cot * attn, axis=0, keepdims=True)
                m["gain_acc"][h] = m["gain_acc"][h] + grad * scaled
                pieces += [m["soft"][h, b, 0:1], delta]
            pieces.append(jnp.zeros((d.stat_rows - len(pieces), BLOCK), F32))
            m["stat"][b] = jnp.concatenate(pieces, axis=0)
            return carry

        lax.fori_loop(0, NB, part_c, 0)
        out_norm = local(m["norm_buf"], norm_hbm, m["out_sem"].at[0])
        out_norm.start()

        for s in range(S):
            for h in range(H):
                m["cot_send"][s, h] = m["cot"][h, q_idx[h][s]]
                m["cst_send"][s, 2 * h : 2 * h + 2] = m["stat"][q_idx[h][s]][2 * h : 2 * h + 2]
            m["cst_send"][s, 2 * H :] = jnp.zeros((d.stat_rows - 2 * H, BLOCK), F32)
        m["gain_mine"][...] = jnp.concatenate(
            [
                jnp.broadcast_to(jnp.sum(m["gain_acc"][h], axis=1, keepdims=True), (W, BLOCK)).T[:8]
                for h in range(H)
            ],
            axis=1,
        )

        def cot_copy(n):
            peer = lax.rem(pos + n, S)
            return remote(m["cot_send"].at[peer], m["cot_recv"].at[pos], m["cot_ss"].at[n], m["cot_rs"].at[n], seq=peer)

        def cst_copy(n):
            peer = lax.rem(pos + n, S)
            return remote(m["cst_send"].at[peer], m["cst_recv"].at[pos], m["cst_ss"].at[n], m["cst_rs"].at[n], seq=peer)

        def gain_copy(n):
            peer = lax.rem(pos + n, S)
            return remote(m["gain_mine"], m["gain_recv"].at[n], m["gain_ss"].at[n], m["gain_rs"].at[n], seq=peer)

        for n in range(1, S):
            cot_copy(n).start()
            cst_copy(n).start()
        own_cot = local(m["cot_send"].at[pos], m["cot_recv"].at[pos], m["own_sem"].at[2])
        own_cst = local(m["cst_send"].at[pos], m["cst_recv"].at[pos], m["own_sem"].at[3])
        own_cot.start()
        own_cst.start()
        for n in range(1, S):
            gain_copy(n).start()

        def terms(keys, values, query, cot, lse, delta):
            prob = jnp.exp2(dot(keys, query, NT) * factor - lse)
            dscore = (prob * (dot(values, cot, NT) - delta)).astype(BF16)
            return prob.astype(BF16), dscore

        def cut_backward(h):
            m["cut_sum"][h] = jnp.zeros((KCUT, BLOCK, 2 * W), F32)

            def step(b, carry):
                query = q[b, :, cols(h)]
                cot = m["cot"][h, b]
                stat = m["stat"][b]
                lse = stat[2 * h : 2 * h + 1]
                delta = stat[2 * h + 1 : 2 * h + 2]
                dq = jnp.zeros((W, BLOCK), F32)
                for c in range(KCUT):
                    keys = m["ck"][h, c * BLOCK : (c + 1) * BLOCK]
                    values = m["cv"][h, c * BLOCK : (c + 1) * BLOCK]
                    prob, dscore = terms(keys, values, query, cot, lse + closed[h][c], delta)
                    dq = dq + dot(keys, dscore, TN)
                    m["cut_sum"][h, c, :, :W] = m["cut_sum"][h, c, :, :W] + dot(dscore, query, NN)
                    m["cut_sum"][h, c, :, W:] = m["cut_sum"][h, c, :, W:] + dot(prob, cot, NN)
                m["acc"][h, b] = dq
                return carry

            lax.fori_loop(0, NB, step, 0)

        def term_of(h, slot):
            c = jnp.int32(0)
            for n in range(KCUT):
                c = jnp.where(cut_dev[h][n] == slot, n, c)
            return c

        def cut_part(h, slot):
            part = m["cut_sum"][h, term_of(h, slot)]
            return jnp.concatenate([part[:, :W] * scale, part[:, W:]], axis=1)

        def x_copy(h):
            return remote(m["x_send"].at[h], m["x_recv"].at[h], m["x_ss"].at[h], m["x_rs"].at[h], seq=o * 2 + 1 - i)

        def z_copy(h, n):
            peer = lax.rem(o + n, L)
            return remote(
                m["z_send"].at[h, peer], m["z_recv"].at[h, n], m["z_ss"].at[h, n], m["z_rs"].at[h, n], seq=peer * 2 + i
            )

        def x_start(h):
            for outer in range(L):
                m["x_send"][h, outer] = cut_part(h, outer * 2 + 1 - i).astype(BF16)
            x_copy(h).start()

        def z_start(h):
            x_copy(h).wait_recv()
            for outer in range(L):
                m["z_send"][h, outer] = (cut_part(h, outer * 2 + i) + m["x_recv"][h, outer].astype(F32)).astype(BF16)
            for n in range(1, L):
                z_copy(h, n).start()

        for h in range(H):
            cut_backward(h)
            x_start(h)

        def near(b, carry):
            stat = m["stat"][b]
            for h in range(H):
                query = q[b, :, cols(h)]
                cot = m["cot"][h, b]
                lse = stat[2 * h : 2 * h + 1]
                delta = stat[2 * h + 1 : 2 * h + 2]
                keys = k[b, :, cols(h)]
                prob, dscore = terms(keys, v[b, :, cols(h)], query, cot, lse, delta)
                dq = m["acc"][h, b] + dot(keys, dscore, TN)
                m["dkv"][b, h, :, :W] = dot(dscore, query, NN) * scale
                m["dkv"][b, h, :, W:] = dot(prob, cot, NN)
                slot = lax.div(perm[h, pos * NB + b], NB)
                keys = m["kv_recv"][slot, h, :, :W]
                prob, dscore = terms(keys, m["kv_recv"][slot, h, :, W:], query, cot, lse, delta)
                dq = dq + dot(keys, dscore, TN)
                m["dq_buf"][b, :, cols(h)] = (dq * scale).T.astype(BF16)
            return carry

        lax.fori_loop(0, NB, near, 0)
        out_dq = local(m["dq_buf"], dq_hbm, m["out_sem"].at[1])
        out_dq.start()
        for h in range(H):
            z_start(h)

        own_q.wait()
        own_cot.wait()
        own_cst.wait()
        for n in range(1, S):
            arrive("q_recv", "q_rs", n)
            arrive("cot_recv", "cot_rs", n)
            arrive("cst_recv", "cst_rs", n)

        def far(b, carry):
            for h in range(H):
                slot = jnp.int32(0)
                for s in range(S):
                    slot = jnp.where(slot_of[h][s] == b, s, slot)
                query = m["q_recv"][slot, h]
                cot = m["cot_recv"][slot, h]
                stat = m["cst_recv"][slot]
                lse = stat[2 * h : 2 * h + 1]
                delta = stat[2 * h + 1 : 2 * h + 2]
                prob, dscore = terms(k[b, :, cols(h)], v[b, :, cols(h)], query, cot, lse, delta)
                m["dkv"][b, h, :, :W] = m["dkv"][b, h, :, :W] + (dot(dscore, query, NN) * scale).astype(BF16).astype(F32)
                m["dkv"][b, h, :, W:] = m["dkv"][b, h, :, W:] + dot(prob, cot, NN).astype(BF16).astype(F32)
            return carry

        lax.fori_loop(0, NB, far, 0)

        gain_total = m["gain_mine"][...]
        for n in range(1, S):
            gain_copy(n).wait_recv()
        for n in range(1, S):
            gain_total = gain_total + m["gain_recv"][n]
        gain_out[...] = gain_total[:1]

        for h in range(H):
            for n in range(1, L):
                z_copy(h, n).wait_recv()
            total = m["z_send"][h, o].astype(F32)
            for n in range(1, L):
                total = total + m["z_recv"][h, n].astype(F32)
            m["cut_sum"][h, 0] = total

        def final(b, carry):
            for h in range(H):
                grad = m["dkv"][b, h]
                hit = jnp.logical_and(cut_has[h] > 0, cut_local[h] == b)
                grad = grad + jnp.where(hit, jnp.float32(1), jnp.float32(0)) * m["cut_sum"][h, 0]
                m["dk_buf"][b, :, cols(h)] = grad[:, :W].astype(BF16)
                m["dv_buf"][b, :, cols(h)] = grad[:, W:].astype(BF16)
            return carry

        lax.fori_loop(0, NB, final, 0)
        out_dk = local(m["dk_buf"], dk_hbm, m["out_sem"].at[2])
        out_dv = local(m["dv_buf"], dv_hbm, m["out_sem"].at[3])
        out_dk.start()
        out_dv.start()

        for t in range(L):

            @pl.when(jnp.logical_and(has_up, o - t >= 0))
            def _(t=t):
                up(t).wait_send()

            @pl.when(jnp.logical_and(has_down, o + t < L))
            def _(t=t):
                down(t).wait_send()

            across(t).wait_send()
        for n in range(1, S):
            kv_copy(n).wait_send()
            q_copy(n).wait_send()
            cot_copy(n).wait_send()
            cst_copy(n).wait_send()
            gain_copy(n).wait_send()
        for n in range(1, HD):
            sum_copy(n).wait_send()
        for h in range(H):
            x_copy(h).wait_send()
            for n in range(1, L):
                z_copy(h, n).wait_send()
        out_norm.wait()
        out_dq.wait()
        out_dk.wait()
        out_dv.wait()

    return kernel


def layer(query_rows, key_rows, value_rows, out_grad, block_perm, cut_count, norm_gain):
    heads = block_perm.shape[0]
    width = query_rows.shape[1] // heads
    d = Dims(
        heads, width, query_rows.shape[0] // BLOCK, lax.axis_size("seq"), lax.axis_size("head")
    )
    scratch = scratch_of(d)
    hbm = pl.BlockSpec(memory_space=pl.ANY)
    smem = pl.BlockSpec(memory_space=pltpu.SMEM)
    vmem = pl.BlockSpec(memory_space=pltpu.VMEM)
    tokens = query_rows.shape[0]
    tiled = (d.blocks, BLOCK, heads * width)
    rows = jax.ShapeDtypeStruct(tiled, BF16)
    outs = pl.pallas_call(
        make_kernel(d, list(scratch)),
        in_specs=[smem, smem, hbm, hbm, hbm, hbm, vmem],
        out_specs=[hbm, hbm, hbm, hbm, vmem],
        out_shape=[rows, rows, rows, rows, jax.ShapeDtypeStruct((1, heads * width), F32)],
        scratch_shapes=list(scratch.values()),
        compiler_params=pltpu.CompilerParams(
            collective_id=0, has_side_effects=True, vmem_limit_bytes=VMEM_LIMIT
        ),
        cost_estimate=pl.CostEstimate(
            flops=int(2 * tokens * BLOCK * heads * width * 44), bytes_accessed=int(16 * tokens * heads * width),
            transcendentals=0,
        ),
        name="layer",
    )(
        block_perm,
        cut_count,
        *[x.reshape(tiled) for x in (query_rows, key_rows, value_rows, out_grad)],
        norm_gain.reshape(1, heads * width),
    )
    return *[x.reshape(tokens, heads * width) for x in outs[:4]], outs[4].reshape(heads * width)


def solution(mesh):
    rows = P("seq", "head")
    return jax.shard_map(
        layer,
        mesh=mesh,
        in_specs=(rows, rows, rows, rows, P("head", None), P("head"), P("head")),
        out_specs=(rows, rows, rows, rows, P("head")),
        check_vma=False,
    )
```

profile of v0, /device:TPU:16, one launch (start us, length us, event | category | flops | bytes accessed | tf_op | source)
XLA Modules:
  0.0 165.1 jit_solution(2816001244977607544)
XLA Ops:
  0.6 157.3 %layer.1 = (bf16[8,256,256]{2,1,0:T(8,128)(2,1)}, bf16[8,256,256]{2,1,0:T(8,128)(2,1)}, bf16[8,256,256]{2,1,0:T(8,128)(2,1)}, bf16[8,256,256]{2,1,0:T(8,128)(2,1)}, f32[1,256]{1,0:T(1,128)}) custom-call(s32[2,64]{1,0:T(2,128)} %perm.1, s32[2]{0:T(128)} %count.1, bf16[8,256,256]{2,1,0:T(8,128)(2,1)} %bitcast.15, bf16[8,256,256]{2,1,0:T(8,128)(2,1)} %bitcast.16, ...), custom_call_target="tpu_custom_call" | custom-call | flops 11811160064 | bytes 8388608 | tf_op jit(solution)/shard_map/layer/pallas_call | solution.py:600
  158.0 0.0 copy-start.2
  158.0 2.4 %copy.17 = bf16[2048,256]{1,0:T(8,128)(2,1)} copy(bf16[2048,256]{1,0:T(8,128)(2,1)} %bitcast.13) | data formatting | bytes 2097152
  160.4 0.0 copy-done.2
  160.4 0.0 copy-start.1
  160.4 1.0 copy.18
  161.3 0.6 copy-done.1
  162.0 0.0 copy-start
  162.0 1.0 copy.19
  162.9 0.6 copy-done
  163.6 0.0 copy-start.3
  163.6 1.0 copy.20
  164.5 0.0 copy-done.3
  164.5 0.6 copy.21
Async XLA Ops:
  158.0 2.4 %copy-start.2 = (bf16[8,256,256]{2,1,0:T(8,128)(2,1)S(1)}, bf16[8,256,256]{2,1,0:T(8,128)(2,1)}, u32[]{:S(2)}) copy-start(bf16[8,256,256]{2,1,0:T(8,128)(2,1)} %get-tuple-element.11) | copy-start | bytes 3145732
  160.4 1.6 copy-start.1
  162.0 1.6 copy-start
  163.6 1.0 copy-start.3
where the time goes:
time: 165 us
  Pallas kernels  157 us (95%)
  local copies, waits for them, and re-layouts  7.1 us (4%)
    pallas_call x1, Pallas kernels, layer(): pl.pallas_call(make_kernel(d, list(scratch)), in_specs=[smem, smem, hbm,...  157 us
    unnamed x13, local copies, waits for them, and re-layouts  7.1 us

commit v1 on v0

--- a/solution.py
+++ b/solution.py
@@ -88,10 +88,10 @@
         cot_rs=dma((S,)),
         cst_ss=dma((S,)),
         cst_rs=dma((S,)),
-        up_ss=dma((L,)),
-        down_ss=dma((L,)),
-        across_ss=dma((L,)),
-        cut_rs=dma((S,)),
+        up_ss=dma((L, H)),
+        down_ss=dma((L, H)),
+        across_ss=dma((L, H)),
+        cut_rs=dma((S, H)),
         sum_ss=dma((d.head_devs,)),
         sum_rs=dma((d.head_devs,)),
         x_ss=dma((H,)),
@@ -187,52 +187,59 @@
             r = cut_local[h]
             m["cut"][pos, h, :, :W] = k[r, :, cols(h)]
             m["cut"][pos, h, :, W:] = v[r, :, cols(h)]
+        pl.semaphore_wait(barrier, S - 1 + HD - 1)
+
+        def cut_copy(h, outer, sem, target):
+            slot = outer * 2 + i
+            return remote(m["cut"].at[slot, h], m["cut"].at[slot, h], sem, m["cut_rs"].at[slot, h], seq=target)
+
+        def cut_arrive(h, slot):
+            remote(
+                m["cut"].at[slot, h], m["cut"].at[slot, h], m["across_ss"].at[0, h], m["cut_rs"].at[slot, h], seq=pos
+            ).wait_recv()
+
+        steps = [L // 2] + [n for n in range(1, L) if n != L // 2]
+        hops = [None] + [(n, 0) for n in steps] + [(n, 1) for n in steps] + [(0, 1)]
+
+        def peer_of(n):
+            return lax.rem(o + hops[n][0], L) * 2 + lax.rem(i + hops[n][1], 2)
+
+        def source_of(n):
+            return lax.rem(o + L - hops[n][0], L) * 2 + lax.rem(i + hops[n][1], 2)
+
+        def kv_copy(n):
+            peer = peer_of(n)
+            return remote(m["kv_send"].at[peer], m["kv_recv"].at[pos], m["kv_ss"].at[n], m["kv_rs"].at[n], seq=peer)
+
+        def q_copy(n):
+            peer = peer_of(n)
+            return remote(m["q_send"].at[peer], m["q_recv"].at[pos], m["q_ss"].at[n], m["q_rs"].at[n], seq=peer)
+
+        def arrive(buf, rs, n):
+            src = source_of(n)
+            remote(m[buf].at[src], m[buf].at[src], m[rs].at[n], m[rs].at[n], seq=src).wait_recv()
+
+        has_up = o + 1 < L
+        has_down = o > 0
+
+        def up(t, h):
+            return cut_copy(h, o - t, m["up_ss"].at[t, h], pos + 2)
+
+        def down(t, h):
+            return cut_copy(h, o + t, m["down_ss"].at[t, h], pos - 2)
+
+        def across(outer, h):
+            return cut_copy(h, outer, m["across_ss"].at[outer, h], o * 2 + 1 - i)
+
+        for h in range(H):
+            pl.when(has_up)(lambda h=h: up(0, h).start())
+            pl.when(has_down)(lambda h=h: down(0, h).start())
+            across(o, h).start()
         for h in range(H):
             for s in range(S):
                 r = kv_idx[h][s]
                 m["kv_send"][s, h, :, :W] = k[r, :, cols(h)]
                 m["kv_send"][s, h, :, W:] = v[r, :, cols(h)]
-        pl.semaphore_wait(barrier, S - 1 + HD - 1)
-
-        def cut_copy(outer, sem, target):
-            slot = outer * 2 + i
-            return remote(m["cut"].at[slot], m["cut"].at[slot], sem, m["cut_rs"].at[slot], seq=target)
-
-        def cut_arrive(slot):
-            remote(m["cut"].at[slot], m["cut"].at[slot], m["across_ss"].at[0], m["cut_rs"].at[slot], seq=pos).wait_recv()
-
-        def kv_copy(n):
-            peer = lax.rem(pos + n, S)
-            return remote(m["kv_send"].at[peer], m["kv_recv"].at[pos], m["kv_ss"].at[n], m["kv_rs"].at[n], seq=peer)
-
-        def q_copy(n):
-            peer = lax.rem(pos + n, S)
-            return remote(m["q_send"].at[peer], m["q_recv"].at[pos], m["q_ss"].at[n], m["q_rs"].at[n], seq=peer)
-
-        def arrive(buf, rs, n):
-            src = lax.rem(pos + S - n, S)
-            remote(m[buf].at[src], m[buf].at[src], m[rs].at[n], m[rs].at[n], seq=src).wait_recv()
-
-        has_up = o + 1 < L
-        has_down = o > 0
-
-        def up(t):
-            return cut_copy(o - t, m["up_ss"].at[t], pos + 2)
-
-        def down(t):
-            return cut_copy(o + t, m["down_ss"].at[t], pos - 2)
-
-        def across(outer):
-            return cut_copy(outer, m["across_ss"].at[outer], o * 2 + 1 - i)
-
-        per = -(-(S - 1) // L)
-        groups = [list(range(1, S))[n * per : (n + 1) * per] for n in range(L)]
-
-        pl.when(has_up)(lambda: up(0).start())
-        pl.when(has_down)(lambda: down(0).start())
-        across(o).start()
-        for n in groups[0]:
-            kv_copy(n).start()
         own_kv = local(m["kv_send"].at[pos], m["kv_recv"].at[pos], m["own_sem"].at[0])
         own_kv.start()
 
@@ -254,28 +261,36 @@
 
         lax.fori_loop(0, NB, turn, 0)
 
+        def send_pairs():
+            for n in range(1, S):
+                kv_copy(n).start()
+            for n in range(1, S):
+                q_copy(n).start()
+
         for t in range(L - 1):
             below = o - 1 - t
             above = o + 1 + t
-
-            @pl.when(below >= 0)
-            def _(below=below, t=t):
-                cut_arrive(below * 2 + i)
-                pl.when(has_up)(lambda: up(t + 1).start())
-                across(below).start()
-
-            @pl.when(above < L)
-            def _(above=above, t=t):
-                cut_arrive(above * 2 + i)
-                pl.when(has_down)(lambda: down(t + 1).start())
-                across(above).start()
-
-            for n in groups[t + 1]:
-                kv_copy(n).start()
-        for n in range(1, S):
-            q_copy(n).start()
+            if t == L - 2:
+                send_pairs()
+            for h in range(H):
+
+                @pl.when(below >= 0)
+                def _(below=below, t=t, h=h):
+                    cut_arrive(h, below * 2 + i)
+                    if t < L - 2:
+                        pl.when(has_up)(lambda: up(t + 1, h).start())
+                    across(below, h).start()
+
+                @pl.when(above < L)
+                def _(above=above, t=t, h=h):
+                    cut_arrive(h, above * 2 + i)
+                    if t < L - 2:
+                        pl.when(has_down)(lambda: down(t + 1, h).start())
+                    across(above, h).start()
+
         for outer in range(L):
-            cut_arrive(outer * 2 + 1 - i)
+            for h in range(H):
+                cut_arrive(h, outer * 2 + 1 - i)
         for h in range(H):
             for c in range(KCUT):
                 m["ck"][h, c * BLOCK : (c + 1) * BLOCK] = m["cut"][cut_dev[h][c], h, :, :W]
@@ -390,15 +405,15 @@
         )
 
         def cot_copy(n):
-            peer = lax.rem(pos + n, S)
+            peer = peer_of(n)
             return remote(m["cot_send"].at[peer], m["cot_recv"].at[pos], m["cot_ss"].at[n], m["cot_rs"].at[n], seq=peer)
 
         def cst_copy(n):
-            peer = lax.rem(pos + n, S)
+            peer = peer_of(n)
             return remote(m["cst_send"].at[peer], m["cst_recv"].at[pos], m["cst_ss"].at[n], m["cst_rs"].at[n], seq=peer)
 
         def gain_copy(n):
-            peer = lax.rem(pos + n, S)
+            peer = peer_of(n)
             return remote(m["gain_mine"], m["gain_recv"].at[n], m["gain_ss"].at[n], m["gain_rs"].at[n], seq=peer)
 
         for n in range(1, S):
@@ -472,6 +487,8 @@
         for h in range(H):
             cut_backward(h)
             x_start(h)
+            if h > 0:
+                z_start(h - 1)
 
         def near(b, carry):
             stat = m["stat"][b]
@@ -495,8 +512,7 @@
         lax.fori_loop(0, NB, near, 0)
         out_dq = local(m["dq_buf"], dq_hbm, m["out_sem"].at[1])
         out_dq.start()
-        for h in range(H):
-            z_start(h)
+        z_start(H - 1)
 
         own_q.wait()
         own_cot.wait()
@@ -553,17 +569,19 @@
         out_dk.start()
         out_dv.start()
 
-        for t in range(L):
-
-            @pl.when(jnp.logical_and(has_up, o - t >= 0))
-            def _(t=t):
-                up(t).wait_send()
-
-            @pl.when(jnp.logical_and(has_down, o + t < L))
-            def _(t=t):
-                down(t).wait_send()
-
-            across(t).wait_send()
+        for h in range(H):
+            for t in range(L - 1):
+
+                @pl.when(jnp.logical_and(has_up, o - t >= 0))
+                def _(t=t, h=h):
+                    up(t, h).wait_send()
+
+                @pl.when(jnp.logical_and(has_down, o + t < L))
+                def _(t=t, h=h):
+                    down(t, h).wait_send()
+
+            for outer in range(L):
+                across(outer, h).wait_send()
         for n in range(1, S):
             kv_copy(n).wait_send()
             q_copy(n).wait_send()
@@ -582,6 +600,26 @@
         out_dv.wait()
 
     return kernel
+
+
+def copy_kernel(*refs):
+    half = len(refs) // 2
+    for src, dst in zip(refs[:half], refs[half:]):
+        dst[...] = src[...]
+
+
+def copies(arrays):
+    blocks, rows, width = arrays[0].shape
+    spec = pl.BlockSpec((blocks // 2, rows, width), lambda n: (n, 0, 0))
+    return pl.pallas_call(
+        copy_kernel,
+        grid=(2,),
+        in_specs=[spec] * len(arrays),
+        out_specs=[spec] * len(arrays),
+        out_shape=[jax.ShapeDtypeStruct(x.shape, x.dtype) for x in arrays],
+        compiler_params=pltpu.CompilerParams(vmem_limit_bytes=VMEM_LIMIT),
+        name="results",
+    )(*arrays)
 
 
 def layer(query_rows, key_rows, value_rows, out_grad, block_perm, cut_count, norm_gain):
@@ -617,7 +655,7 @@
         *[x.reshape(tiled) for x in (query_rows, key_rows, value_rows, out_grad)],
         norm_gain.reshape(1, heads * width),
     )
-    return *[x.reshape(tokens, heads * width) for x in outs[:4]], outs[4].reshape(heads * width)
+    return *[x.reshape(tokens, heads * width) for x in copies(outs[:4])], outs[4].reshape(heads * width)
 
 
 def solution(mesh):

time: 165 us -> 147 us (0.89); the launches traced: 165 us -> 145 us
  Pallas kernels: 157 us -> 143 us
  local copies, waits for them, and re-layouts: 7.1 us -> 1.24 us
    pallas_call x1, Pallas kernels: 157 us -> 140 us  [layer(): pl.pallas_call(make_kernel(d, list(scratch)), in_specs=[smem, smem, hbm,...]
    unnamed x13 -> x3, local copies, waits for them, and re-layouts: 7.1 us -> 1.24 us
    pallas_call x0 -> x1, Pallas kernels: none -> 3.67 us  [copies(): pl.pallas_call(copy_kernel, grid=(2,), in_specs=[spec] * len(arrays), out...]
where the time goes in v1:
time: 147 us; the launch traced here: 145 us
  Pallas kernels  143 us (97%)
    pallas_call x1, Pallas kernels, layer(): pl.pallas_call(make_kernel(d, list(scratch)), in_specs=[smem, smem, hbm,...  140 us
    pallas_call x1, Pallas kernels, copies(): pl.pallas_call(copy_kernel, grid=(2,), in_specs=[spec] * len(arrays), out...  3.67 us

profile of v1, /device:TPU:16, one launch (start us, length us, event | category | flops | bytes accessed | tf_op | source)
XLA Modules:
  0.0 145.1 jit_solution(13582384437363925833)
XLA Ops:
  0.6 139.5 %layer.1 = (bf16[8,256,256]{2,1,0:T(8,128)(2,1)}, bf16[8,256,256]{2,1,0:T(8,128)(2,1)}, bf16[8,256,256]{2,1,0:T(8,128)(2,1)}, bf16[8,256,256]{2,1,0:T(8,128)(2,1)}, f32[1,256]{1,0:T(1,128)}) custom-call(s32[2,64]{1,0:T(2,128)} %perm.1, s32[2]{0:T(128)} %count.1, bf16[8,256,256]{2,1,0:T(8,128)(2,1)} %bitcast.11, bf16[8,256,256]{2,1,0:T(8,128)(2,1)} %bitcast.12, ...), custom_call_target="tpu_custom_call" | custom-call | flops 11811160064 | bytes 8388608 | tf_op jit(solution)/shard_map/layer/pallas_call | solution.py:638
  140.1 3.7 %results.1 = (bf16[8,256,256]{2,1,0:T(8,128)(2,1)}, bf16[8,256,256]{2,1,0:T(8,128)(2,1)}, bf16[8,256,256]{2,1,0:T(8,128)(2,1)}, bf16[8,256,256]{2,1,0:T(8,128)(2,1)}) custom-call(bf16[8,256,256]{2,1,0:T(8,128)(2,1)} %get-tuple-element.14.refs_0_, bf16[8,256,256]{2,1,0:T(8,128)(2,1)} %get-tuple-element.15.refs_1_, ...), custom_call_target="tpu_custom_call" | custom-call | tf_op jit(solution)/shard_map/results/pallas_call | solution.py:614
  143.8 0.0 copy-start
  143.8 0.7 copy-done
  144.5 0.6 copy.13
Async XLA Ops:
  143.8 0.7 copy-start
